TPU v7x, 32 devices: a whole 2x2x4 slice. The times are simulated.
32 devices in a mesh: dp: 8 (over y, x, core), tensor: 4 (over z).
Axes of the slice: x: 2, y: 2, z: 4, core: 2. Of those that a mesh axis runs over, the one named last changes fastest.
Arguments:
- tokens: bfloat16 [8192, 1280], P(('dp', 'tensor')), may hold values from -6 to 6
- w_query: bfloat16 [1280, 1280], P('dp', 'tensor'), may hold values from -0.15625 to 0.15625
- w_key: bfloat16 [1280, 1280], P('dp', 'tensor'), may hold values from -0.15625 to 0.15625
- w_value: bfloat16 [1280, 1280], P('dp', 'tensor'), may hold values from -0.15625 to 0.15625
- w_out: bfloat16 [1280, 1280], P('dp', 'tensor'), may hold values from -0.15625 to 0.15625
- w_up: bfloat16 [1280, 5120], P('dp', 'tensor'), may hold values from -0.15625 to 0.15625
- w_gate: bfloat16 [1280, 5120], P('dp', 'tensor'), may hold values from -0.15625 to 0.15625
- w_down: bfloat16 [1280, 5120], P('dp', 'tensor'), may hold values from -0.078125 to 0.078125
- qk_scale: float32 [1280], P('tensor'), may hold values from 0.8 to 1.8
- up_scale: float32 [5120], P('tensor'), may hold values from 0.5 to 2
- gate_scale: float32 [5120], P('tensor'), may hold values from 0.5 to 2
- alpha_attn: float32 [1280], replicated, may hold values from 0.2 to 0.6
- alpha_mlp: float32 [1280], replicated, may hold values from 0.2 to 0.6
- cotangent: bfloat16 [8192, 1280], P(('dp', 'tensor')), may hold values from -6 to 6
Outputs:
- output: bfloat16 [8192, 1280], P(('dp', 'tensor'))
- tokens_gradient: float32 [8192, 1280], P(('dp', 'tensor'))
- w_query_gradient: float32 [1280, 1280], P('dp', 'tensor')
- w_key_gradient: float32 [1280, 1280], P('dp', 'tensor')
- w_value_gradient: float32 [1280, 1280], P('dp', 'tensor')
- w_out_gradient: float32 [1280, 1280], P('dp', 'tensor')
- w_up_gradient: float32 [1280, 5120], P('dp', 'tensor')
- w_gate_gradient: float32 [1280, 5120], P('dp', 'tensor')
- w_down_gradient: float32 [1280, 5120], P('dp', 'tensor')
- qk_scale_gradient: float32 [1280], P('tensor')
- up_scale_gradient: float32 [5120], P('tensor')
- gate_scale_gradient: float32 [5120], P('tensor')
- alpha_attn_gradient: float32 [1280], replicated
- alpha_mlp_gradient: float32 [1280], replicated
All inputs are finite; a program needn't handle non-finite values.
Results may differ from a plain program's by a relative error of at most 0.017.
Values may be sent and summed in bfloat16 or wider, within the bound.
A program may use at most 192 MiB of HBM per device.

v0:
```python
import jax
import jax.numpy as jnp
from jax import lax
from jax.sharding import PartitionSpec as P

HEAD_DIM = 64
HIGH = lax.Precision.HIGHEST
EPS = 1e-06


def unit_rows(value):
    scale = lax.rsqrt(jnp.mean(value * value, axis=-1, keepdims=True) + EPS)
    return (value * scale, scale)


def unit_back(grad, unit, scale):
    return scale * (grad - unit * jnp.mean(grad * unit, axis=-1, keepdims=True))


def contract_rows(left, right):
    return lax.dot_general(
        left, right, (((0,), (0,)), ((), ())), preferred_element_type=jnp.float32
    )


def contract_cols(left, right):
    return lax.dot_general(
        left, right, (((1,), (1,)), ((), ())), preferred_element_type=jnp.float32
    )


def tables(width, length):
    half_dim = HEAD_DIM // 2
    column = lax.iota(jnp.int32, width)
    within = column % HEAD_DIM
    freq_index = (within % half_dim).astype(jnp.float32)
    frequency = 10000.0 ** (-freq_index / half_dim)
    position = lax.iota(jnp.float32, length)
    angle = position[:, None] * frequency[None, :]
    first_half = (within < half_dim)[None, :]
    heads = width // HEAD_DIM
    member = (
        lax.broadcasted_iota(jnp.int32, (width, heads), 0) // HEAD_DIM
        == lax.broadcasted_iota(jnp.int32, (width, heads), 1)
    ).astype(jnp.float32)
    return (jnp.cos(angle), jnp.sin(angle), first_half, member)


def rope_apply(value, cosine, sine, first_half):
    half_dim = HEAD_DIM // 2
    turned = jnp.where(
        first_half, -jnp.roll(value, -half_dim, axis=1), jnp.roll(value, half_dim, axis=1)
    )
    return value * cosine + turned * sine


def rope_back(grad, cosine, sine, first_half):
    half_dim = HEAD_DIM // 2
    weighted = grad * sine
    turned = jnp.where(
        first_half, jnp.roll(weighted, -half_dim, axis=1), -jnp.roll(weighted, half_dim, axis=1)
    )
    return grad * cosine + turned


def head_unit(value, member):
    mean_sq = (
        jnp.dot(value * value, member, precision=HIGH, preferred_element_type=jnp.float32)
        / HEAD_DIM
    )
    scale = jnp.dot(
        lax.rsqrt(mean_sq + EPS), member.T, precision=HIGH, preferred_element_type=jnp.float32
    )
    return (value * scale, scale)


def head_back(grad, unit, scale, member):
    inner = (
        jnp.dot(grad * unit, member, precision=HIGH, preferred_element_type=jnp.float32) / HEAD_DIM
    )
    spread = jnp.dot(inner, member.T, precision=HIGH, preferred_element_type=jnp.float32)
    return scale * (grad - unit * spread)


def block_scores(query3, key3, start, stop, block):
    scale = HEAD_DIM ** (-0.5)
    scores = (
        jnp.einsum(
            "qhd,khd->hqk", query3[start:stop], key3[:stop], preferred_element_type=jnp.float32
        )
        * scale
    )
    allowed = start + lax.broadcasted_iota(jnp.int32, (block, stop), 0) >= lax.broadcasted_iota(
        jnp.int32, (block, stop), 1
    )
    return jnp.where(allowed[None], scores, -jnp.inf)


def attend(query3, key3, value3, block):
    length = query3.shape[0]
    outputs = []
    totals = []
    for block_id in range(length // block):
        start = block_id * block
        stop = start + block
        scores = block_scores(query3, key3, start, stop, block)
        row_max = jnp.max(scores, axis=-1, keepdims=True)
        log_total = jnp.log(jnp.sum(jnp.exp(scores - row_max), axis=-1, keepdims=True)) + row_max
        weights = jnp.exp(scores - log_total).astype(jnp.bfloat16)
        outputs.append(
            jnp.einsum("hqk,khd->qhd", weights, value3[:stop], preferred_element_type=jnp.float32)
        )
        totals.append(log_total)
    return (jnp.concatenate(outputs, axis=0), totals)


def attend_back(query3, key3, value3, grad3, totals, block):
    length = query3.shape[0]
    scale = HEAD_DIM ** (-0.5)
    query_parts = []
    key_grad = jnp.zeros(key3.shape, jnp.float32)
    value_grad = jnp.zeros(value3.shape, jnp.float32)
    for block_id in range(length // block):
        start = block_id * block
        stop = start + block
        scores = block_scores(query3, key3, start, stop, block)
        probs = jnp.exp(scores - totals[block_id])
        g_probs = jnp.einsum(
            "qhd,khd->hqk", grad3[start:stop], value3[:stop], preferred_element_type=jnp.float32
        )
        inner = jnp.sum(probs * g_probs, axis=-1, keepdims=True)
        g_scores = (probs * (g_probs - inner)).astype(jnp.bfloat16)
        query_parts.append(
            jnp.einsum("hqk,khd->qhd", g_scores, key3[:stop], preferred_element_type=jnp.float32)
            * scale
        )
        key_grad = key_grad.at[:stop].add(
            jnp.einsum(
                "hqk,qhd->khd", g_scores, query3[start:stop], preferred_element_type=jnp.float32
            )
            * scale
        )
        value_grad = value_grad.at[:stop].add(
            jnp.einsum(
                "hqk,qhd->khd",
                probs.astype(jnp.bfloat16),
                grad3[start:stop],
                preferred_element_type=jnp.float32,
            )
        )
    return (jnp.concatenate(query_parts, axis=0), key_grad, value_grad)


def gather_attention(w_query, w_key, w_value, w_out):
    return (
        lax.all_gather(w_query, "dp", axis=0, tiled=True),
        lax.all_gather(w_key, "dp", axis=0, tiled=True),
        lax.all_gather(w_value, "dp", axis=0, tiled=True),
        lax.all_gather(w_out, "dp", axis=0, tiled=True),
    )


def gather_feedforward(w_up, w_gate, w_down):
    return (
        lax.all_gather(w_up, "dp", axis=0, tiled=True),
        lax.all_gather(w_gate, "dp", axis=0, tiled=True),
        lax.all_gather(w_down, "dp", axis=0, tiled=True),
    )


def on_device(
    tokens,
    w_query,
    w_key,
    w_value,
    w_out,
    w_up,
    w_gate,
    w_down,
    qk_scale,
    up_scale,
    gate_scale,
    alpha_attn,
    alpha_mlp,
    cotangent,
):
    query_w, key_w, value_w, out_w = gather_attention(w_query, w_key, w_value, w_out)
    whole = lax.all_gather(tokens, "tensor", axis=0, tiled=True)
    length = whole.shape[0]
    width = query_w.shape[1]
    block = min(512, length)
    cosine, sine, first_half, member = tables(width, length)
    shape3 = (length, width // HEAD_DIM, HEAD_DIM)
    q_raw = jnp.dot(whole, query_w, preferred_element_type=jnp.float32)
    k_raw = jnp.dot(whole, key_w, preferred_element_type=jnp.float32)
    value_low = jnp.dot(whole, value_w, preferred_element_type=jnp.float32).astype(jnp.bfloat16)
    q_unit, q_norm = head_unit(rope_apply(q_raw, cosine, sine, first_half), member)
    k_unit, k_norm = head_unit(rope_apply(k_raw, cosine, sine, first_half), member)
    query_low = (q_unit * qk_scale).astype(jnp.bfloat16)
    key_low = (k_unit * qk_scale).astype(jnp.bfloat16)
    query3 = query_low.reshape(shape3)
    key3 = key_low.reshape(shape3)
    value3 = value_low.reshape(shape3)
    attended, totals = attend(query3, key3, value3, block)
    attended_low = attended.reshape(length, width).astype(jnp.bfloat16)
    attn_sum = lax.psum_scatter(
        contract_cols(attended_low, out_w), "tensor", scatter_dimension=0, tiled=True
    )
    attn_unit, attn_norm = unit_rows(attn_sum)
    residual = tokens.astype(jnp.float32)
    mid, mid_norm = unit_rows(residual + alpha_attn * (attn_unit - residual))
    mid_low = mid.astype(jnp.bfloat16)
    up_w, gate_w, down_w = gather_feedforward(w_up, w_gate, w_down)
    mid_whole = lax.all_gather(mid_low, "tensor", axis=0, tiled=True)
    up_sum = jnp.dot(mid_whole, up_w, preferred_element_type=jnp.float32)
    gate_sum = jnp.dot(mid_whole, gate_w, preferred_element_type=jnp.float32)
    up_val = up_sum * up_scale
    gate_val = gate_sum * gate_scale
    sigma = jax.nn.sigmoid(gate_val)
    hidden_low = (up_val * (gate_val * sigma)).astype(jnp.bfloat16)
    mlp_sum = lax.psum_scatter(
        contract_cols(hidden_low, down_w), "tensor", scatter_dimension=0, tiled=True
    )
    mlp_unit, mlp_norm = unit_rows(mlp_sum)
    final, final_norm = unit_rows(mid + alpha_mlp * (mlp_unit - mid))
    output = final.astype(jnp.bfloat16)
    g_second = unit_back(cotangent.astype(jnp.float32), final, final_norm)
    g_alpha_mlp = jnp.sum((mlp_unit - mid) * g_second, axis=0)
    g_mlp_low = unit_back(alpha_mlp * g_second, mlp_unit, mlp_norm).astype(jnp.bfloat16)
    up_w, gate_w, down_w = gather_feedforward(w_up, w_gate, w_down)
    g_mlp_whole = lax.all_gather(g_mlp_low, "tensor", axis=0, tiled=True)
    down_grad = contract_rows(g_mlp_whole, hidden_low)
    g_hidden = jnp.dot(g_mlp_whole, down_w, preferred_element_type=jnp.float32)
    g_up = g_hidden * (gate_val * sigma)
    g_gate = g_hidden * up_val * (sigma * (1.0 + gate_val * (1.0 - sigma)))
    up_scale_grad = jnp.sum(g_up * up_sum, axis=0)
    gate_scale_grad = jnp.sum(g_gate * gate_sum, axis=0)
    g_up_low = (g_up * up_scale).astype(jnp.bfloat16)
    g_gate_low = (g_gate * gate_scale).astype(jnp.bfloat16)
    up_grad = contract_rows(mid_whole, g_up_low)
    gate_grad = contract_rows(mid_whole, g_gate_low)
    g_mid_part = contract_cols(g_up_low, up_w) + contract_cols(g_gate_low, gate_w)
    g_mid = (1.0 - alpha_mlp) * g_second + lax.psum_scatter(
        g_mid_part, "tensor", scatter_dimension=0, tiled=True
    )
    up_grad, gate_grad, down_grad = (
        lax.psum_scatter(up_grad, "dp", scatter_dimension=0, tiled=True),
        lax.psum_scatter(gate_grad, "dp", scatter_dimension=0, tiled=True),
        lax.psum_scatter(down_grad, "dp", scatter_dimension=0, tiled=True),
    )
    g_first = unit_back(g_mid, mid, mid_norm)
    g_alpha_attn = jnp.sum((attn_unit - residual) * g_first, axis=0)
    g_attn_low = unit_back(alpha_attn * g_first, attn_unit, attn_norm).astype(jnp.bfloat16)
    query_w, key_w, value_w, out_w = gather_attention(w_query, w_key, w_value, w_out)
    g_attn_whole = lax.all_gather(g_attn_low, "tensor", axis=0, tiled=True)
    out_grad = contract_rows(g_attn_whole, attended_low)
    g_attended_low = jnp.dot(g_attn_whole, out_w, preferred_element_type=jnp.float32).astype(
        jnp.bfloat16
    )
    g_query3, g_key3, g_value3 = attend_back(
        query3, key3, value3, g_attended_low.reshape(shape3), totals, block
    )
    g_query = g_query3.reshape(length, width)
    g_key = g_key3.reshape(length, width)
    qk_grad = jnp.sum(g_query * q_unit, axis=0) + jnp.sum(g_key * k_unit, axis=0)
    g_q_raw_low = rope_back(
        head_back(g_query * qk_scale, q_unit, q_norm, member), cosine, sine, first_half
    ).astype(jnp.bfloat16)
    g_k_raw_low = rope_back(
        head_back(g_key * qk_scale, k_unit, k_norm, member), cosine, sine, first_half
    ).astype(jnp.bfloat16)
    g_value_low = g_value3.reshape(length, width).astype(jnp.bfloat16)
    query_grad = contract_rows(whole, g_q_raw_low)
    key_grad = contract_rows(whole, g_k_raw_low)
    value_grad = contract_rows(whole, g_value_low)
    g_tok_part = (
        contract_cols(g_q_raw_low, query_w)
        + contract_cols(g_k_raw_low, key_w)
        + contract_cols(g_value_low, value_w)
    )
    tokens_grad = (1.0 - alpha_attn) * g_first + lax.psum_scatter(
        g_tok_part.astype(jnp.bfloat16), "tensor", scatter_dimension=0, tiled=True
    ).astype(jnp.float32)
    query_grad, key_grad, value_grad, out_grad = (
        lax.psum_scatter(query_grad, "dp", scatter_dimension=0, tiled=True),
        lax.psum_scatter(key_grad, "dp", scatter_dimension=0, tiled=True),
        lax.psum_scatter(value_grad, "dp", scatter_dimension=0, tiled=True),
        lax.psum_scatter(out_grad, "dp", scatter_dimension=0, tiled=True),
    )
    qk_grad, up_scale_grad, gate_scale_grad = lax.psum(
        (qk_grad, up_scale_grad, gate_scale_grad), "dp"
    )
    g_alpha_attn, g_alpha_mlp = lax.psum((g_alpha_attn, g_alpha_mlp), ("dp", "tensor"))
    return (
        output,
        tokens_grad,
        query_grad,
        key_grad,
        value_grad,
        out_grad,
        up_grad,
        gate_grad,
        down_grad,
        qk_grad,
        up_scale_grad,
        gate_scale_grad,
        g_alpha_attn,
        g_alpha_mlp,
    )


def solution(mesh):
    in_specs = (
        P(("dp", "tensor"), None),
        P("dp", "tensor"),
        P("dp", "tensor"),
        P("dp", "tensor"),
        P("dp", "tensor"),
        P("dp", "tensor"),
        P("dp", "tensor"),
        P("dp", "tensor"),
        P("tensor"),
        P("tensor"),
        P("tensor"),
        P(),
        P(),
        P(("dp", "tensor"), None),
    )
    out_specs = (
        P(("dp", "tensor"), None),
        P(("dp", "tensor"), None),
        P("dp", "tensor"),
        P("dp", "tensor"),
        P("dp", "tensor"),
        P("dp", "tensor"),
        P("dp", "tensor"),
        P("dp", "tensor"),
        P("dp", "tensor"),
        P("tensor"),
        P("tensor"),
        P("tensor"),
        P(),
        P(),
    )
    return jax.shard_map(
        on_device, mesh=mesh, in_specs=in_specs, out_specs=out_specs, check_vma=False
    )
```

profile of v0, /device:TPU:0, one launch (start us, length us, event | category | flops | bytes accessed | tf_op | source)
XLA Modules:
  0.0 1157.3 jit_solution(15452497443347139287)
XLA Ops:
  9.0 12.8 %all_gather.41 = bf16[1280,320]{1,0:T(8,128)(2,1)S(1)} all-gather(bf16[160,320]{1,0:T(8,128)(2,1)} %param.29), channel_id=1, replica_groups=mesh['dp'=8,'tensor'=4] {'dp'}, dimensions={0}, use_global_device_ids=true | all-gather | bytes 921600 | tf_op jit(solution)/shard_map/all_gather | solution.py:158
  21.8 11.6 %all_gather.43 = bf16[1280,320]{1,0:T(8,128)(2,1)} all-gather(bf16[160,320]{1,0:T(8,128)(2,1)S(1)} %copy-done.50), channel_id=1, replica_groups=mesh['dp'=8,'tensor'=4] {'dp'}, dimensions={0}, use_global_device_ids=true | all-gather | bytes 921600 | tf_op jit(solution)/shard_map/all_gather | solution.py:157
  33.3 11.4 all_gather.42
  44.7 11.5 all_gather.44
  56.6 11.3 all-gather.8.cloned.1.call-done
  67.9 3.0 fusion.124
  74.3 6.5 fusion.20
  89.5 3.1 exponential_reduce_fusion
  96.0 2.9 fusion.67
  101.9 3.9 fusion.125
  106.4 92.1 %reduce-scatter.18.cloned.1.call-done = f32[256,1280]{1,0:T(8,128)} async-done(((f32[1024,1280]{1,0:T(8,128)}), f32[256,1280]{1,0:T(8,128)}) %reduce-scatter.18.cloned.1.call-update) | async-done | bytes 1310736 | tf_op jit(solution)/shard_map/reduce_scatter | solution.py:206
  204.5 53.4 %all-gather.10.cloned.1.call-done = bf16[1024,1280]{1,0:T(8,128)(2,1)} async-done(((bf16[256,1280]{1,0:T(8,128)(2,1)}), bf16[1024,1280]{1,0:T(8,128)(2,1)}) %all-gather.10.cloned.1.call-update) | async-done | bytes 2621456 | tf_op jit(solution)/shard_map/all_gather | solution.py:214
  257.8 8.6 fusion.126
  266.4 24.5 %all-gather.12.cloned.1.call-done = bf16[1280,1280]{1,0:T(8,128)(2,1)} async-done(((bf16[160,1280]{1,0:T(8,128)(2,1)}), bf16[1280,1280]{1,0:T(8,128)(2,1)}) %all-gather.12.cloned.1.call-update) | async-done | bytes 3276816 | tf_op jit(solution)/shard_map/all_gather | solution.py:165
  290.8 11.3 multiply_convert_fusion.4
  302.1 23.2 %all-gather.16.cloned.1.call-done = bf16[1280,1280]{1,0:T(8,128)(2,1)} async-done(((bf16[160,1280]{1,0:T(8,128)(2,1)}), bf16[1280,1280]{1,0:T(8,128)(2,1)}) %all-gather.16.cloned.1.call-update) | async-done | bytes 3276816 | tf_op jit(solution)/shard_map/all_gather | solution.py:167
  325.4 8.7 fusion.127
  334.1 93.9 %reduce-scatter.20.cloned.1.call-done = f32[256,1280]{1,0:T(8,128)} async-done(((f32[1024,1280]{1,0:T(8,128)}), f32[256,1280]{1,0:T(8,128)}) %reduce-scatter.20.cloned.1.call-update) | async-done | bytes 1310736 | tf_op jit(solution)/shard_map/reduce_scatter | solution.py:221
  435.4 54.5 %all-gather.18.cloned.1.call-done = bf16[1024,1280]{1,0:T(8,128)(2,1)} async-done(((bf16[256,1280]{1,0:T(8,128)(2,1)}), bf16[1024,1280]{1,0:T(8,128)(2,1)}) %all-gather.18.cloned.1.call-update) | async-done | bytes 2621456 | tf_op jit(solution)/shard_map/all_gather | solution.py:231
  490.0 11.1 multiply_reduce_fusion.1
  501.1 3.6 fusion.128
  505.5 5.4 convolution_add_fusion
  511.0 92.5 %reduce-scatter.22.cloned.1.call-done = f32[256,1280]{1,0:T(8,128)} async-done(((f32[1024,1280]{1,0:T(8,128)}), f32[256,1280]{1,0:T(8,128)}) %reduce-scatter.22.cloned.1.call-update) | async-done | bytes 1310736 | tf_op jit(solution)/shard_map/reduce_scatter | solution.py:243
  610.8 54.8 %all-gather.20.cloned.1.call-done = bf16[1024,1280]{1,0:T(8,128)(2,1)} async-done(((bf16[256,1280]{1,0:T(8,128)(2,1)}), bf16[1024,1280]{1,0:T(8,128)(2,1)}) %all-gather.20.cloned.1.call-update) | async-done | bytes 2621456 | tf_op jit(solution)/shard_map/all_gather | solution.py:255
  669.1 4.5 multiply_reduce_fusion.3
  673.7 4.2 multiply_convert_fusion.1
  680.1 3.9 multiply_reduce_fusion
  683.9 3.3 multiply_convert_fusion
  695.2 7.2 fusion.35
  705.3 6.0 fusion.24
  714.6 3.0 fusion.12
  718.4 3.3 add_convert_fusion
  721.9 8.9 fusion.132
  731.0 9.7 fusion.68
  740.8 8.8 fusion.133
  750.7 4.0 convolution_bitcast_fusion.2
  758.6 3.9 convolution_bitcast_fusion.1
  762.5 2.8 copy.48
  766.4 3.9 convolution_bitcast_fusion
  774.2 4.6 fusion.131
  778.8 39.5 %all-reduce.2 = (f32[1280]{0:T(1024)}, f32[1280]{0:T(1024)}) all-reduce(f32[1280]{0:T(1024)S(1)} %get-tuple-element.110, f32[1280]{0:T(1024)S(1)} %get-tuple-element.108), channel_id=1, replica_groups=mesh['dp'=8,'tensor'=4] {'dp','tensor'}, use_global_device_ids=true, to_apply=%region_33.34 | all-reduce | flops 2560 | bytes 20480 | tf_op jit(solution)/shard_map/psum | solution.py:293
  820.3 25.1 %all-reduce.3 = (f32[320]{0:T(512)}, f32[1280]{0:T(1024)}, f32[1280]{0:T(1024)}) all-reduce(f32[320]{0:T(512)S(1)} %add.253, f32[1280]{0:T(1024)S(1)} %get-tuple-element.107, f32[1280]{0:T(1024)S(1)} %get-tuple-element.106), channel_id=1, replica_groups=mesh['dp'=8,'tensor'=4] {'dp'}, use_global_device_ids=true, to_apply=%region_27.28 | all-reduce | flops 2880 | bytes 23040 | tf_op jit(solution)/shard_map/psum | solution.py:290
  847.7 59.1 %reduce-scatter.30.cloned.1.call-done = f32[160,1280]{1,0:T(8,128)} async-done(((f32[1280,1280]{1,0:T(8,128)}), f32[160,1280]{1,0:T(8,128)}) %reduce-scatter.30.cloned.1.call-update) | async-done | bytes 819216 | tf_op jit(solution)/shard_map/reduce_scatter | solution.py:248
  906.8 66.9 %reduce-scatter.32.cloned.1.call-done = f32[160,1280]{1,0:T(8,128)} async-done(((f32[1280,1280]{1,0:T(8,128)}), f32[160,1280]{1,0:T(8,128)}) %reduce-scatter.32.cloned.1.call-update) | async-done | bytes 819216 | tf_op jit(solution)/shard_map/reduce_scatter | solution.py:249
  973.7 43.9 %reduce-scatter.34.cloned.1.call-done = f32[160,320]{1,0:T(8,128)} async-done(((f32[1280,320]{1,0:T(8,128)}), f32[160,320]{1,0:T(8,128)}) %reduce-scatter.34.cloned.1.call-update) | async-done | bytes 204816
  1017.6 44.1 %reduce-scatter.36.cloned.1.call-done = f32[160,320]{1,0:T(8,128)} async-done(((f32[1280,320]{1,0:T(8,128)}), f32[160,320]{1,0:T(8,128)}) %reduce-scatter.36.cloned.1.call-update) | async-done | bytes 204816
  1061.7 43.9 %reduce-scatter.38.cloned.1.call-done = f32[160,320]{1,0:T(8,128)} async-done(((f32[1280,320]{1,0:T(8,128)}), f32[160,320]{1,0:T(8,128)}) %reduce-scatter.38.cloned.1.call-update) | async-done | bytes 204816
  1105.6 44.1 %reduce-scatter.26.cloned.1.call-done = f32[160,320]{1,0:T(8,128)} async-done(((f32[1280,320]{1,0:T(8,128)}), f32[160,320]{1,0:T(8,128)}) %reduce-scatter.26.cloned.1.call-update) | async-done | bytes 204816 | tf_op jit(solution)/shard_map/reduce_scatter | solution.py:288
  (244 shorter events, 76.4 us)
Async XLA Ops:
  8.0 13.7 %copy-start.50 = (bf16[160,320]{1,0:T(8,128)(2,1)S(1)}, bf16[160,320]{1,0:T(8,128)(2,1)}, u32[]{:S(2)}) copy-start(bf16[160,320]{1,0:T(8,128)(2,1)} %param.28) | copy-start | bytes 307204
  8.0 25.3 %copy-start.51 = (bf16[160,320]{1,0:T(8,128)(2,1)S(1)}, bf16[160,320]{1,0:T(8,128)(2,1)}, u32[]{:S(2)}) copy-start(bf16[160,320]{1,0:T(8,128)(2,1)} %param.27) | copy-start | bytes 307204
  8.0 59.9 %all-gather.8.cloned.1.call-start = ((), (), s32[]{:S(2)}) async-start(), calls=%async_computation.11 | async-start | bytes 3276800 | tf_op jit(solution)/shard_map/all_gather | solution.py:188
  8.8 189.7 %reduce-scatter.18.cloned.1.call-start = ((), (), s32[]{:S(2)}) async-start(), calls=%async_computation.12 | async-start | bytes 6553600 | tf_op jit(solution)/shard_map/reduce_scatter | solution.py:206
  9.0 35.8 %copy-start.52 = (bf16[160,320]{1,0:T(8,128)(2,1)S(1)}, bf16[160,320]{1,0:T(8,128)(2,1)}, u32[]{:S(2)}) copy-start(bf16[160,320]{1,0:T(8,128)(2,1)} %param.30) | copy-start | bytes 307204
  21.8 70.9 %copy-start.24 = (bf16[1280,320]{1,0:T(8,128)(2,1)}, bf16[1280,320]{1,0:T(8,128)(2,1)S(1)}, u32[]{:S(2)}) copy-start(bf16[1280,320]{1,0:T(8,128)(2,1)S(1)} %all_gather.41) | copy-start | bytes 2457604
  83.3 4.2 copy-start.10
  87.5 6.3 copy-start.33
  87.5 6.3 copy-start.35
  89.5 6.5 copy-start
  93.8 5.1 copy-start.42
  94.9 4.1 copy-start.1
  105.8 94.3 %copy-start.49 = (f32[1280]{0:T(1024)S(1)}, f32[1280]{0:T(1024)}, u32[]{:S(2)}) copy-start(f32[1280]{0:T(1024)} %param.37) | copy-start | bytes 15364
  105.8 98.7 %all-gather.14.cloned.1.call-start = ((), (), s32[]{:S(2)}) async-start(), calls=%async_computation.15 | async-start | bytes 3686400 | tf_op jit(solution)/shard_map/all_gather | solution.py:166
  106.4 151.4 %all-gather.10.cloned.1.call-start = ((), (), s32[]{:S(2)}) async-start(), calls=%async_computation.13 | async-start | bytes 3276800 | tf_op jit(solution)/shard_map/all_gather | solution.py:214
  202.8 88.0 %all-gather.12.cloned.1.call-start = ((), (), s32[]{:S(2)}) async-start(), calls=%async_computation.14 | async-start | bytes 3686400 | tf_op jit(solution)/shard_map/all_gather | solution.py:165
  203.4 122.0 %all-gather.16.cloned.1.call-start = ((), (), s32[]{:S(2)}) async-start(), calls=%async_computation.16 | async-start | bytes 3686400 | tf_op jit(solution)/shard_map/all_gather | solution.py:167
  204.1 86.7 %copy-start.57 = (f32[1280]{0:T(1024)S(1)}, f32[1280]{0:T(1024)}, u32[]{:S(2)}) copy-start(f32[1280]{0:T(1024)} %param.35) | copy-start | bytes 15364
  204.1 86.7 %copy-start.58 = (f32[1280]{0:T(1024)S(1)}, f32[1280]{0:T(1024)}, u32[]{:S(2)}) copy-start(f32[1280]{0:T(1024)} %param.36) | copy-start | bytes 15364
  204.1 223.9 %reduce-scatter.20.cloned.1.call-start = ((), (), s32[]{:S(2)}) async-start(), calls=%async_computation.17 | async-start | bytes 6553600 | tf_op jit(solution)/shard_map/reduce_scatter | solution.py:221
  334.1 95.6 %copy-start.48 = (f32[1280]{0:T(1024)S(1)}, f32[1280]{0:T(1024)}, u32[]{:S(2)}) copy-start(f32[1280]{0:T(1024)} %param.38) | copy-start | bytes 15364
  334.1 155.9 %all-gather.18.cloned.1.call-start = ((), (), s32[]{:S(2)}) async-start(), calls=%async_computation.18 | async-start | bytes 3276800 | tf_op jit(solution)/shard_map/all_gather | solution.py:231
  434.9 168.5 %reduce-scatter.22.cloned.1.call-start = ((), (), s32[]{:S(2)}) async-start(), calls=%async_computation.19 | async-start | bytes 6553600 | tf_op jit(solution)/shard_map/reduce_scatter | solution.py:243
  490.0 11.1 copy-start.55
  501.1 3.6 copy-start.60
  501.1 3.8 copy-start.59
  501.1 4.4 copy-start.54
  510.9 154.7 %all-gather.20.cloned.1.call-start = ((), (), s32[]{:S(2)}) async-start(), calls=%async_computation.20 | async-start | bytes 3276800 | tf_op jit(solution)/shard_map/all_gather | solution.py:255
  609.4 56.2 %copy-start.30 = (bf16[1280,320]{1,0:T(8,128)(2,1)S(1)}, bf16[1280,320]{1,0:T(8,128)(2,1)}, u32[]{:S(2)}) copy-start(bf16[1280,320]{1,0:T(8,128)(2,1)} %all_gather.44) | copy-start | bytes 2457604
  610.5 58.6 %copy-start.43 = (bf16[512,320]{0,1:T(8,128)(2,1)S(1)}, bf16[512,320]{0,1:T(8,128)(2,1)}, u32[]{:S(2)}) copy-start(bf16[512,320]{0,1:T(8,128)(2,1)} %copy-done.42) | copy-start | bytes 983044
  610.5 234.9 %reduce-scatter.24.cloned.1.call-start = ((), (), s32[]{:S(2)}) async-start(), calls=%async_computation.21 | async-start | bytes 3276800 | tf_op jit(solution)/shard_map/reduce_scatter | solution.py:281
  669.1 4.5 copy-start.40
  669.1 10.7 slice-start
  669.1 10.7 slice-start.1
  673.7 4.2 copy-start.36
  673.7 6.1 slice-start.2
  683.9 3.3 copy-start.15
  695.2 7.7 slice-start.3
  705.3 6.0 copy-start.28
  714.6 3.9 copy-start.25
  721.8 125.9 %reduce-scatter.28.cloned.1.call-start = ((), (), s32[]{:S(2)}) async-start(), calls=%async_computation.23 | async-start | bytes 7372800 | tf_op jit(solution)/shard_map/reduce_scatter | solution.py:247
  730.8 176.0 %reduce-scatter.30.cloned.1.call-start = ((), (), s32[]{:S(2)}) async-start(), calls=%async_computation.24 | async-start | bytes 7372800 | tf_op jit(solution)/shard_map/reduce_scatter | solution.py:248
  740.7 233.0 %reduce-scatter.32.cloned.1.call-start = ((), (), s32[]{:S(2)}) async-start(), calls=%async_computation.25 | async-start | bytes 7372800 | tf_op jit(solution)/shard_map/reduce_scatter | solution.py:249
  749.6 268.0 %reduce-scatter.34.cloned.1.call-start = ((), (), s32[]{:S(2)}) async-start(), calls=%async_computation.26 | async-start | bytes 2211840
  757.5 304.2 %reduce-scatter.36.cloned.1.call-start = ((), (), s32[]{:S(2)}) async-start(), calls=%async_computation.27 | async-start | bytes 2211840
  765.3 340.3 %reduce-scatter.38.cloned.1.call-start = ((), (), s32[]{:S(2)}) async-start(), calls=%async_computation.28 | async-start | bytes 2211840
  773.1 376.6 %reduce-scatter.26.cloned.1.call-start = ((), (), s32[]{:S(2)}) async-start(), calls=%async_computation.22 | async-start | bytes 2211840 | tf_op jit(solution)/shard_map/reduce_scatter | solution.py:288
  820.0 25.4 %copy-start.13 = (f32[256,1280]{1,0:T(8,128)S(1)}, f32[256,1280]{1,0:T(8,128)}, u32[]{:S(2)}) copy-start(f32[256,1280]{1,0:T(8,128)} %copy-done.12) | copy-start | bytes 3932164
  (36 other events, 56.8 us)
Sparse Core Ops, SparseCore 0:
  10.4 57.4 all-gather.7
  105.9 92.5 reduce-scatter.17
  334.2 93.7 reduce-scatter.19
  511.0 92.3 reduce-scatter.21
Sparse Core Ops, SparseCore 1:
  108.2 31.4 all-gather.13
  202.9 54.9 all-gather.9
  259.6 31.2 all-gather.11
  292.7 32.6 all-gather.15
  435.0 54.9 all-gather.17
  610.6 54.9 all-gather.19
  721.9 50.8 reduce-scatter.23
  776.6 63.3 reduce-scatter.27
  843.9 62.9 reduce-scatter.29
  910.8 62.8 reduce-scatter.31
  977.6 40.0 reduce-scatter.33
  1021.6 40.0 reduce-scatter.35
  1065.6 40.0 reduce-scatter.37
  1109.6 40.0 reduce-scatter.25
where the time goes:
time: 1160 us
  waiting for transfers between devices  805 us (69%)
  matrix products  153 us (13%)
  blocking collectives  112 us (10%)
  other arithmetic  43.9 us (4%)
  local copies, waits for them, and re-layouts  24.4 us (2%)
  between operations  16.9 us (1%)
    unnamed x21, waiting for transfers between devices  135 us
    reduce_scatter x1, waiting for transfers between devices, on_device(): lax.psum_scatter(contract_cols(hidden_low, down_w), 'tensor', scatter_dim...  93.9 us
    reduce_scatter x1, waiting for transfers between devices, on_device(): lax.psum_scatter(g_mid_part, 'tensor', scatter_dimension=0, tiled=True)  92.5 us
    reduce_scatter x1, waiting for transfers between devices, on_device(): lax.psum_scatter(contract_cols(attended_low, out_w), 'tensor', scatter_di...  92.1 us
    reduce_scatter x1, waiting for transfers between devices, on_device(): lax.psum_scatter(down_grad, 'dp', scatter_dimension=0, tiled=True)  66.9 us
    reduce_scatter x1, waiting for transfers between devices, on_device(): lax.psum_scatter(gate_grad, 'dp', scatter_dimension=0, tiled=True)  59.1 us
    all_gather x1, waiting for transfers between devices, on_device(): g_attn_whole = lax.all_gather(g_attn_low, 'tensor', axis=0, tiled=True)  54.8 us
    all_gather x1, waiting for transfers between devices, on_device(): g_mlp_whole = lax.all_gather(g_mlp_low, 'tensor', axis=0, tiled=True)  54.5 us
  transfers between devices with their start and end apart: 18, of which 15 were waited for; matrix products, arithmetic and copies ran while one was open for 7% of the time, Pallas kernels for 0%

commit v1 on v0

--- a/solution.py
+++ b/solution.py
@@ -6,6 +6,27 @@
 HEAD_DIM = 64
 HIGH = lax.Precision.HIGHEST
 EPS = 1e-06
+
+
+def joined_along(blocks, dim):
+    blocks = jnp.moveaxis(blocks, 0, dim)
+    shape = blocks.shape
+    return blocks.reshape(*shape[:dim], shape[dim] * shape[dim + 1], *shape[dim + 2 :])
+
+
+def doubled(array, axis):
+    peers, index = (lax.axis_size(axis), lax.axis_index(axis))
+    blocks, apart = (array[None], 1)
+    while apart < peers:
+        other = lax.ppermute(blocks, axis, [(i, i ^ apart) for i in range(peers)])
+        low = index & apart == 0
+        blocks = jnp.concatenate([jnp.where(low, blocks, other), jnp.where(low, other, blocks)])
+        apart *= 2
+    return blocks
+
+
+def gather_by_bits(shard, axis, dim):
+    return joined_along(doubled(shard, axis), dim)
 
 
 def unit_rows(value):
@@ -252,7 +273,7 @@
     g_alpha_attn = jnp.sum((attn_unit - residual) * g_first, axis=0)
     g_attn_low = unit_back(alpha_attn * g_first, attn_unit, attn_norm).astype(jnp.bfloat16)
     query_w, key_w, value_w, out_w = gather_attention(w_query, w_key, w_value, w_out)
-    g_attn_whole = lax.all_gather(g_attn_low, "tensor", axis=0, tiled=True)
+    g_attn_whole = gather_by_bits(g_attn_low, "tensor", 0)
     out_grad = contract_rows(g_attn_whole, attended_low)
     g_attended_low = jnp.dot(g_attn_whole, out_w, preferred_element_type=jnp.float32).astype(
         jnp.bfloat16

time: 1160 us -> 1190 us (1.026)
  waiting for transfers between devices: 805 us -> 821 us
    ppermute x0 -> x2, waiting for transfers between devices: none -> 71 us  [doubled(): other = lax.ppermute(blocks, axis, [(i, i ^ apart) for i in range(peers)])]
    all_gather x1 -> x0, waiting for transfers between devices: 54.8 us -> none  [on_device(): g_attn_whole = lax.all_gather(g_attn_low, 'tensor', axis=0, tiled=True)]
    unnamed x135 -> x173, local copies, waits for them, and re-layouts: 22.6 us -> 26.4 us
    unnamed x21 -> x20, waiting for transfers between devices: 135 us -> 135 us
  transfers between devices with their start and end apart: 18 -> 19, of which waited for: 15 -> 16; matrix products, arithmetic and copies ran while one was open for 7% -> 7% of each run, Pallas kernels for 0% -> 0%
where the time goes in v1:
time: 1190 us
  waiting for transfers between devices  821 us (69%)
  matrix products  155 us (13%)
  blocking collectives  111 us (9%)
  other arithmetic  47.3 us (4%)
  local copies, waits for them, and re-layouts  28.2 us (2%)
  between operations  16.9 us (1%)
    unnamed x20, waiting for transfers between devices  135 us
    reduce_scatter x1, waiting for transfers between devices, on_device(): lax.psum_scatter(contract_cols(hidden_low, down_w), 'tensor', scatter_dim...  93.9 us
    reduce_scatter x1, waiting for transfers between devices, on_device(): lax.psum_scatter(g_mid_part, 'tensor', scatter_dimension=0, tiled=True)  92.5 us
    reduce_scatter x1, waiting for transfers between devices, on_device(): lax.psum_scatter(contract_cols(attended_low, out_w), 'tensor', scatter_di...  92.1 us
    ppermute x2, waiting for transfers between devices, doubled(): other = lax.ppermute(blocks, axis, [(i, i ^ apart) for i in range(peers)])  71 us
    reduce_scatter x1, waiting for transfers between devices, on_device(): lax.psum_scatter(down_grad, 'dp', scatter_dimension=0, tiled=True)  66.8 us
    reduce_scatter x1, waiting for transfers between devices, on_device(): lax.psum_scatter(gate_grad, 'dp', scatter_dimension=0, tiled=True)  58.9 us
    all_gather x1, waiting for transfers between devices, on_device(): g_mlp_whole = lax.all_gather(g_mlp_low, 'tensor', axis=0, tiled=True)  54.6 us
  transfers between devices with their start and end apart: 19, of which 16 were waited for; matrix products, arithmetic and copies ran while one was open for 7% of the time, Pallas kernels for 0%

profile of v1, /device:TPU:0, one launch (start us, length us, event | category | flops | bytes accessed | tf_op | source)
XLA Modules:
  0.0 1185.6 jit_solution(11223314024236230291)
XLA Ops:
  9.0 12.7 %all_gather.38 = bf16[1280,320]{1,0:T(8,128)(2,1)S(1)} all-gather(bf16[160,320]{1,0:T(8,128)(2,1)} %param.29), channel_id=1, replica_groups=mesh['dp'=8,'tensor'=4] {'dp'}, dimensions={0}, use_global_device_ids=true | all-gather | bytes 921600 | tf_op jit(solution)/shard_map/all_gather | solution.py:179
  21.7 10.9 all_gather.40
  32.5 11.4 all_gather.39
  44.0 11.5 all_gather.41
  55.8 12.1 %all-gather.7.cloned.1.call-done = bf16[1024,1280]{1,0:T(8,128)(2,1)} async-done(((bf16[256,1280]{1,0:T(8,128)(2,1)}), bf16[1024,1280]{1,0:T(8,128)(2,1)}) %all-gather.7.cloned.1.call-update) | async-done | bytes 2621456 | tf_op jit(solution)/shard_map/all_gather | solution.py:209
  74.1 6.9 fusion.20
  85.0 2.9 multiply_convert_fusion.7
  90.0 3.1 exponential_reduce_fusion
  96.5 2.9 convolution_convert_fusion.2
  102.3 3.9 fusion.129
  106.8 92.1 %reduce-scatter.18.cloned.1.call-done = f32[256,1280]{1,0:T(8,128)} async-done(((f32[1024,1280]{1,0:T(8,128)}), f32[256,1280]{1,0:T(8,128)}) %reduce-scatter.18.cloned.1.call-update) | async-done | bytes 1310736 | tf_op jit(solution)/shard_map/reduce_scatter | solution.py:227
  204.8 53.4 %all-gather.9.cloned.1.call-done = bf16[1024,1280]{1,0:T(8,128)(2,1)} async-done(((bf16[256,1280]{1,0:T(8,128)(2,1)}), bf16[1024,1280]{1,0:T(8,128)(2,1)}) %all-gather.9.cloned.1.call-update) | async-done | bytes 2621456 | tf_op jit(solution)/shard_map/all_gather | solution.py:235
  258.2 8.6 fusion.130
  266.8 24.4 %all-gather.11.cloned.1.call-done = bf16[1280,1280]{1,0:T(8,128)(2,1)} async-done(((bf16[160,1280]{1,0:T(8,128)(2,1)}), bf16[1280,1280]{1,0:T(8,128)(2,1)}) %all-gather.11.cloned.1.call-update) | async-done | bytes 3276816 | tf_op jit(solution)/shard_map/all_gather | solution.py:186
  291.2 11.3 multiply_convert_fusion.4
  302.5 23.2 %all-gather.15.cloned.1.call-done = bf16[1280,1280]{1,0:T(8,128)(2,1)} async-done(((bf16[160,1280]{1,0:T(8,128)(2,1)}), bf16[1280,1280]{1,0:T(8,128)(2,1)}) %all-gather.15.cloned.1.call-update) | async-done | bytes 3276816 | tf_op jit(solution)/shard_map/all_gather | solution.py:188
  325.8 8.6 fusion.131
  334.4 93.9 %reduce-scatter.20.cloned.1.call-done = f32[256,1280]{1,0:T(8,128)} async-done(((f32[1024,1280]{1,0:T(8,128)}), f32[256,1280]{1,0:T(8,128)}) %reduce-scatter.20.cloned.1.call-update) | async-done | bytes 1310736 | tf_op jit(solution)/shard_map/reduce_scatter | solution.py:242
  436.3 54.6 %all-gather.17.cloned.1.call-done = bf16[1024,1280]{1,0:T(8,128)(2,1)} async-done(((bf16[256,1280]{1,0:T(8,128)(2,1)}), bf16[1024,1280]{1,0:T(8,128)(2,1)}) %all-gather.17.cloned.1.call-update) | async-done | bytes 2621456 | tf_op jit(solution)/shard_map/all_gather | solution.py:252
  490.9 11.7 multiply_reduce_fusion.1
  502.6 3.6 fusion.132
  506.9 5.4 convolution_add_fusion
  512.4 92.5 %reduce-scatter.22.cloned.1.call-done = f32[256,1280]{1,0:T(8,128)} async-done(((f32[1024,1280]{1,0:T(8,128)}), f32[256,1280]{1,0:T(8,128)}) %reduce-scatter.22.cloned.1.call-update) | async-done | bytes 1310736 | tf_op jit(solution)/shard_map/reduce_scatter | solution.py:264
  611.5 14.9 %collective-permute-done = bf16[1,256,1280]{2,1,0:T(8,128)(2,1)S(1)} collective-permute-done((bf16[1,256,1280]{2,1,0:T(8,128)(2,1)S(1)}, bf16[1,256,1280]{2,1,0:T(8,128)(2,1)S(1)}, u32[]{:S(2)}, u32[]{:S(2)}) %collective-permute-start) | collective-permute-done | bytes 655392 | tf_op jit(solution)/shard_map/ppermute | solution.py:21
  627.8 3.0 collective-permute-start.1
  630.8 56.1 %collective-permute-done.1 = bf16[2,256,1280]{2,1,0:T(8,128)(2,1)} collective-permute-done((bf16[2,256,1280]{2,1,0:T(8,128)(2,1)S(1)}, bf16[2,256,1280]{2,1,0:T(8,128)(2,1)}, u32[]{:S(2)}, u32[]{:S(2)}) %collective-permute-start.1) | collective-permute-done | bytes 1310752 | tf_op jit(solution)/shard_map/ppermute | solution.py:21
  694.1 2.8 multiply_convert_fusion.1
  699.7 6.4 multiply_reduce_fusion
  706.1 6.1 multiply_convert_fusion
  721.8 7.4 fusion.35
  732.8 5.6 fusion.24
  741.7 3.0 fusion.12
  745.5 3.3 add_convert_fusion
  749.4 8.8 fusion.135
  758.9 9.7 fusion.66
  768.6 8.9 fusion.136
  778.6 4.0 convolution_bitcast_fusion.2
  786.4 3.9 convolution_bitcast_fusion.1
  794.3 3.9 convolution_bitcast_fusion
  802.1 4.6 fusion.68
  807.4 39.4 %all-reduce.2 = (f32[1280]{0:T(1024)}, f32[1280]{0:T(1024)}) all-reduce(f32[1280]{0:T(1024)S(1)} %copy-done.62, f32[1280]{0:T(1024)S(1)} %copy-done.61), channel_id=1, replica_groups=mesh['dp'=8,'tensor'=4] {'dp','tensor'}, use_global_device_ids=true, to_apply=%region_33.34 | all-reduce | flops 2560 | bytes 20480 | tf_op jit(solution)/shard_map/psum | solution.py:314
  849.2 25.0 %all-reduce.3 = (f32[320]{0:T(512)}, f32[1280]{0:T(1024)}, f32[1280]{0:T(1024)}) all-reduce(f32[320]{0:T(512)S(1)} %add.253, f32[1280]{0:T(1024)S(1)} %copy-done.68, f32[1280]{0:T(1024)S(1)} %copy-done.67), channel_id=1, replica_groups=mesh['dp'=8,'tensor'=4] {'dp'}, use_global_device_ids=true, to_apply=%region_27.28 | all-reduce | flops 2880 | bytes 23040 | tf_op jit(solution)/shard_map/psum | solution.py:311
  876.5 58.9 %reduce-scatter.30.cloned.1.call-done = f32[160,1280]{1,0:T(8,128)} async-done(((f32[1280,1280]{1,0:T(8,128)}), f32[160,1280]{1,0:T(8,128)}) %reduce-scatter.30.cloned.1.call-update) | async-done | bytes 819216 | tf_op jit(solution)/shard_map/reduce_scatter | solution.py:269
  935.4 66.8 %reduce-scatter.32.cloned.1.call-done = f32[160,1280]{1,0:T(8,128)} async-done(((f32[1280,1280]{1,0:T(8,128)}), f32[160,1280]{1,0:T(8,128)}) %reduce-scatter.32.cloned.1.call-update) | async-done | bytes 819216 | tf_op jit(solution)/shard_map/reduce_scatter | solution.py:270
  1002.1 44.1 %reduce-scatter.34.cloned.1.call-done = f32[160,320]{1,0:T(8,128)} async-done(((f32[1280,320]{1,0:T(8,128)}), f32[160,320]{1,0:T(8,128)}) %reduce-scatter.34.cloned.1.call-update) | async-done | bytes 204816
  1046.2 43.9 %reduce-scatter.36.cloned.1.call-done = f32[160,320]{1,0:T(8,128)} async-done(((f32[1280,320]{1,0:T(8,128)}), f32[160,320]{1,0:T(8,128)}) %reduce-scatter.36.cloned.1.call-update) | async-done | bytes 204816
  1090.1 44.1 %reduce-scatter.38.cloned.1.call-done = f32[160,320]{1,0:T(8,128)} async-done(((f32[1280,320]{1,0:T(8,128)}), f32[160,320]{1,0:T(8,128)}) %reduce-scatter.38.cloned.1.call-update) | async-done | bytes 204816
  1134.2 43.9 %reduce-scatter.26.cloned.1.call-done = f32[160,320]{1,0:T(8,128)} async-done(((f32[1280,320]{1,0:T(8,128)}), f32[160,320]{1,0:T(8,128)}) %reduce-scatter.26.cloned.1.call-update) | async-done | bytes 204816 | tf_op jit(solution)/shard_map/reduce_scatter | solution.py:309
  (287 shorter events, 88.9 us)
Async XLA Ops:
  8.0 13.7 %copy-start.57 = (bf16[160,320]{1,0:T(8,128)(2,1)S(1)}, bf16[160,320]{1,0:T(8,128)(2,1)}, u32[]{:S(2)}) copy-start(bf16[160,320]{1,0:T(8,128)(2,1)} %param.28) | copy-start | bytes 307204
  8.0 59.9 %all-gather.7.cloned.1.call-start = ((), (), s32[]{:S(2)}) async-start(), calls=%async_computation.11 | async-start | bytes 3276800 | tf_op jit(solution)/shard_map/all_gather | solution.py:209
  8.8 23.8 %copy-start.58 = (bf16[160,320]{1,0:T(8,128)(2,1)S(1)}, bf16[160,320]{1,0:T(8,128)(2,1)}, u32[]{:S(2)}) copy-start(bf16[160,320]{1,0:T(8,128)(2,1)} %param.27) | copy-start | bytes 307204
  8.8 190.1 %reduce-scatter.18.cloned.1.call-start = ((), (), s32[]{:S(2)}) async-start(), calls=%async_computation.12 | async-start | bytes 6553600 | tf_op jit(solution)/shard_map/reduce_scatter | solution.py:227
  8.8 65.3 %copy-start.69 = (pred[320]{0:T(512)(128)(4,1)}, pred[320]{0:T(512)(128)(4,1)S(1)}, u32[]{:S(2)}) copy-start(pred[320]{0:T(512)(128)(4,1)S(1)} %fusion.108) | copy-start | bytes 964
  8.8 76.1 %copy-start.63 = (pred[320]{0:T(512)(128)(4,1)}, pred[320]{0:T(512)(128)(4,1)S(1)}, u32[]{:S(2)}) copy-start(pred[320]{0:T(512)(128)(4,1)S(1)} %fusion.110) | copy-start | bytes 964
  8.9 65.2 %copy-start.65 = (f32[320]{0:T(512)}, f32[320]{0:T(512)S(1)}, u32[]{:S(2)}) copy-start(f32[320]{0:T(512)S(1)} %fusion.104) | copy-start | bytes 3844
  9.0 682.6 %copy-start.16 = (pred[512,512]{0,1:T(8,128)(4,1)}, pred[512,512]{0,1:T(8,128)(4,1)S(1)}, u32[]{:S(2)}) copy-start(pred[512,512]{0,1:T(8,128)(4,1)S(1)} %iota_compare_fusion.1) | copy-start | bytes 786436
  21.7 71.4 %copy-start.25 = (bf16[1280,320]{1,0:T(8,128)(2,1)}, bf16[1280,320]{1,0:T(8,128)(2,1)S(1)}, u32[]{:S(2)}) copy-start(bf16[1280,320]{1,0:T(8,128)(2,1)S(1)} %all_gather.38) | copy-start | bytes 2457604
  21.7 22.3 %copy-start.59 = (bf16[160,320]{1,0:T(8,128)(2,1)S(1)}, bf16[160,320]{1,0:T(8,128)(2,1)}, u32[]{:S(2)}) copy-start(bf16[160,320]{1,0:T(8,128)(2,1)} %param.30) | copy-start | bytes 307204
  32.5 35.4 %copy-start.27 = (bf16[1280,320]{1,0:T(8,128)(2,1)}, bf16[1280,320]{1,0:T(8,128)(2,1)S(1)}, u32[]{:S(2)}) copy-start(bf16[1280,320]{1,0:T(8,128)(2,1)S(1)} %all_gather.40) | copy-start | bytes 2457604
  83.4 4.5 copy-start.10
  88.0 6.3 copy-start.35
  88.0 6.3 copy-start.37
  90.0 6.5 copy-start
  94.3 5.2 copy-start.45
  95.3 4.1 copy-start.1
  106.2 94.3 %copy-start.56 = (f32[1280]{0:T(1024)S(1)}, f32[1280]{0:T(1024)}, u32[]{:S(2)}) copy-start(f32[1280]{0:T(1024)} %param.37) | copy-start | bytes 15364
  106.2 98.6 %all-gather.13.cloned.1.call-start = ((), (), s32[]{:S(2)}) async-start(), calls=%async_computation.15 | async-start | bytes 3686400 | tf_op jit(solution)/shard_map/all_gather | solution.py:187
  106.8 151.4 %all-gather.9.cloned.1.call-start = ((), (), s32[]{:S(2)}) async-start(), calls=%async_computation.13 | async-start | bytes 3276800 | tf_op jit(solution)/shard_map/all_gather | solution.py:235
  203.2 88.0 %all-gather.11.cloned.1.call-start = ((), (), s32[]{:S(2)}) async-start(), calls=%async_computation.14 | async-start | bytes 3686400 | tf_op jit(solution)/shard_map/all_gather | solution.py:186
  203.8 122.0 %all-gather.15.cloned.1.call-start = ((), (), s32[]{:S(2)}) async-start(), calls=%async_computation.16 | async-start | bytes 3686400 | tf_op jit(solution)/shard_map/all_gather | solution.py:188
  204.5 86.7 %copy-start.74 = (f32[1280]{0:T(1024)S(1)}, f32[1280]{0:T(1024)}, u32[]{:S(2)}) copy-start(f32[1280]{0:T(1024)} %param.35) | copy-start | bytes 15364
  204.5 86.7 %copy-start.75 = (f32[1280]{0:T(1024)S(1)}, f32[1280]{0:T(1024)}, u32[]{:S(2)}) copy-start(f32[1280]{0:T(1024)} %param.36) | copy-start | bytes 15364
  204.5 223.8 %reduce-scatter.20.cloned.1.call-start = ((), (), s32[]{:S(2)}) async-start(), calls=%async_computation.17 | async-start | bytes 6553600 | tf_op jit(solution)/shard_map/reduce_scatter | solution.py:242
  334.3 95.6 %copy-start.55 = (f32[1280]{0:T(1024)S(1)}, f32[1280]{0:T(1024)}, u32[]{:S(2)}) copy-start(f32[1280]{0:T(1024)} %param.38) | copy-start | bytes 15364
  334.4 156.5 %all-gather.17.cloned.1.call-start = ((), (), s32[]{:S(2)}) async-start(), calls=%async_computation.18 | async-start | bytes 3276800 | tf_op jit(solution)/shard_map/all_gather | solution.py:252
  435.8 169.1 %reduce-scatter.22.cloned.1.call-start = ((), (), s32[]{:S(2)}) async-start(), calls=%async_computation.19 | async-start | bytes 6553600 | tf_op jit(solution)/shard_map/reduce_scatter | solution.py:264
  490.9 11.7 copy-start.72
  502.5 4.4 copy-start.71
  512.3 361.9 %reduce-scatter.24.cloned.1.call-start = ((), (), s32[]{:S(2)}) async-start(), calls=%async_computation.20 | async-start | bytes 3276800 | tf_op jit(solution)/shard_map/reduce_scatter | solution.py:302
  610.0 16.4 %collective-permute-start = (bf16[1,256,1280]{2,1,0:T(8,128)(2,1)S(1)}, bf16[1,256,1280]{2,1,0:T(8,128)(2,1)S(1)}, u32[]{:S(2)}, u32[]{:S(2)}) collective-permute-start(bf16[1,256,1280]{2,1,0:T(8,128)(2,1)S(1)} %fusion.67), channel_id=1, source_target_pairs={{0,1},{1,0},{2,3},{3,2},{4,5},{5,4},{6,7},{7,6},{8,9},{9,8},{10,11... | collective-permute-start | bytes 1966088 | tf_op jit(solution)/shard_map/ppermute | solution.py:21
  627.8 59.1 %collective-permute-start.1 = (bf16[2,256,1280]{2,1,0:T(8,128)(2,1)S(1)}, bf16[2,256,1280]{2,1,0:T(8,128)(2,1)}, u32[]{:S(2)}, u32[]{:S(2)}) collective-permute-start(bf16[2,256,1280]{2,1,0:T(8,128)(2,1)S(1)} %pad_maximum_fusion.1), channel_id=1, source_target_pairs={{0,2},{1,3},{2,0},{3,1},{4,6},{5,7},{6,4},{7,5},{8,10},{9,11},{10,... | collective-permute-start | bytes 3932168 | tf_op jit(solution)/shard_map/ppermute | solution.py:21
  686.8 4.8 slice-start.3
  691.9 7.5 slice-start
  691.9 7.6 slice-start.1
  694.1 5.4 slice-start.2
  706.1 6.1 copy-start.15
  732.8 5.6 copy-start.30
  741.7 3.9 copy-start.26
  748.9 127.6 %reduce-scatter.28.cloned.1.call-start = ((), (), s32[]{:S(2)}) async-start(), calls=%async_computation.22 | async-start | bytes 7372800 | tf_op jit(solution)/shard_map/reduce_scatter | solution.py:268
  758.2 177.1 %reduce-scatter.30.cloned.1.call-start = ((), (), s32[]{:S(2)}) async-start(), calls=%async_computation.23 | async-start | bytes 7372800 | tf_op jit(solution)/shard_map/reduce_scatter | solution.py:269
  768.6 233.5 %reduce-scatter.32.cloned.1.call-start = ((), (), s32[]{:S(2)}) async-start(), calls=%async_computation.24 | async-start | bytes 7372800 | tf_op jit(solution)/shard_map/reduce_scatter | solution.py:270
  777.5 268.7 %reduce-scatter.34.cloned.1.call-start = ((), (), s32[]{:S(2)}) async-start(), calls=%async_computation.25 | async-start | bytes 2211840
  785.4 304.7 %reduce-scatter.36.cloned.1.call-start = ((), (), s32[]{:S(2)}) async-start(), calls=%async_computation.26 | async-start | bytes 2211840
  793.2 341.0 %reduce-scatter.38.cloned.1.call-start = ((), (), s32[]{:S(2)}) async-start(), calls=%async_computation.27 | async-start | bytes 2211840
  801.0 377.1 %reduce-scatter.26.cloned.1.call-start = ((), (), s32[]{:S(2)}) async-start(), calls=%async_computation.21 | async-start | bytes 2211840 | tf_op jit(solution)/shard_map/reduce_scatter | solution.py:309
  848.5 25.7 %copy-start.13 = (f32[256,1280]{1,0:T(8,128)S(1)}, f32[256,1280]{1,0:T(8,128)}, u32[]{:S(2)}) copy-start(f32[256,1280]{1,0:T(8,128)} %copy-done.12) | copy-start | bytes 3932164
  (56 other events, 89.8 us)
Sparse Core Ops, SparseCore 0:
  10.4 57.4 all-gather.6
  106.3 92.5 reduce-scatter.17
  334.5 93.7 reduce-scatter.19
  512.5 92.3 reduce-scatter.21
Sparse Core Ops, SparseCore 1:
  108.6 31.4 all-gather.12
  203.3 54.9 all-gather.8
  260.0 31.2 all-gather.10
  293.1 32.6 all-gather.14
  435.9 54.9 all-gather.16
  749.0 52.3 reduce-scatter.23
  805.2 63.3 reduce-scatter.27
  872.4 62.8 reduce-scatter.29
  939.3 62.8 reduce-scatter.31
  1006.1 40.0 reduce-scatter.33
  1050.1 40.0 reduce-scatter.35
  1094.1 40.0 reduce-scatter.37
  1138.0 40.0 reduce-scatter.25
